TPU v7x, 32 devices: a whole 2x2x4 slice. The times are simulated.
32 devices in a mesh: samp: 8 (over z, y), gene: 4 (over x, core).
Axes of the slice: x: 2, y: 2, z: 4, core: 2. Of those that a mesh axis runs over, the one named last changes fastest.
Arguments:
- genotypes: int32 [256, 4096], P('samp', 'gene'), may hold values from -2147483648 to 1789569706, as said below
- allele_freq: float32 [4096], P('gene'), may hold values from 0.035 to 0.56
- sample_weight: float32 [16, 256], P(None, 'samp'), may hold values from 0.2 to 2
- residual: float32 [16, 256], P(None, 'samp'), may hold values from -12 to 12
- variant_weight: float32 [4096], P('gene'), may hold values from 0.2 to 4
- block_gene: int32 [32], replicated, may hold values from 0 to 15, as said below
- gene_variants: int32 [16], replicated, may hold values from 1 to 384, as said below
Outputs:
- burden_z: float32 [16], replicated
- skat_z: float32 [16], replicated
Inputs may be any that keep to these rules, and one draw needn't show every extreme that they name: Each word holds 16 dosages 0, 1 or 2: bits 2k and 2k+1 of genotypes[i, v] are the dosage of variant slot v in sample (k, i); a dosage 2 in the top field sets the sign bit. `block_gene`: never falling; the blocks come in aligned groups of four, each shared by two consecutive genes, so every gene has 1 to 3 blocks. `gene_variants`: A gene with m blocks has from (m - 1) * 128 + 1 to m * 128 live variants; the slots after them in its last block are padding.
All inputs are finite; a program needn't handle non-finite values.
Results may differ from a plain program's by a relative error of at most 0.0037.
Values sent between devices are 32-bit elements; how exact they have to be, the bound alone decides.
A program may use at most 64 MiB of HBM per device.

v0:
```python
import jax
import jax.numpy as jnp
from jax import lax
from jax.sharding import PartitionSpec as P

BLK = 128


def unpack(packed_words, allele_part, root_weight):
    fields = root_weight.shape[0]
    offsets = 2 * jnp.arange(fields, dtype=jnp.int32)
    dosage = jnp.bitwise_and(jnp.right_shift(packed_words[None, :, :], offsets[:, None, None]), 3)
    centered = dosage.astype(jnp.float32) - 2.0 * allele_part[None, None, :]
    return (root_weight[:, :, None] * centered).astype(jnp.bfloat16)


def block_grams(scaled, block_count):
    stacked = scaled.reshape(scaled.shape[0] * scaled.shape[1], block_count, BLK)
    return jnp.einsum("sbu,sbv->buv", stacked, stacked, preferred_element_type=jnp.float32)


def block_stats(gram_part, scores, effective):
    weighted_score = effective * scores
    burden_sum = jnp.sum(weighted_score, axis=1)
    skat_sum = jnp.sum(weighted_score * weighted_score, axis=1)
    image = jnp.einsum("buv,bv->bu", gram_part, effective, precision=lax.Precision.HIGHEST)
    burden_var = jnp.sum(effective * image, axis=1)
    diagonal = jnp.diagonal(gram_part, axis1=1, axis2=2)
    trace_one = jnp.sum(effective * effective * diagonal, axis=1)
    scaled_gram = effective[:, :, None] * gram_part * effective[:, None, :]
    trace_two = jnp.sum(scaled_gram * scaled_gram, axis=(1, 2))
    return jnp.stack([burden_sum, burden_var, skat_sum, trace_one, trace_two])


def live_weights(block_ids, variant_part, block_gene, gene_variants):
    total_blocks = block_gene.shape[0]
    genes = gene_variants.shape[0]
    chosen = block_ids[:, None] == jnp.arange(total_blocks, dtype=jnp.int32)[None, :]
    gene_of = jnp.sum(jnp.where(chosen, block_gene[None, :], 0), axis=1)
    first_block = jnp.sum((block_gene[None, :] < gene_of[:, None]).astype(jnp.int32), axis=1)
    member = gene_of[:, None] == jnp.arange(genes, dtype=jnp.int32)[None, :]
    counted = jnp.sum(jnp.where(member, gene_variants[None, :], 0), axis=1)
    column = jnp.arange(BLK, dtype=jnp.int32)
    is_live = (block_ids - first_block)[:, None] * BLK + column[None, :] < counted[:, None]
    return (variant_part * is_live.astype(jnp.float32), member.astype(jnp.float32))


def local(
    genotypes, allele_freq, sample_weight, residual, variant_weight, block_gene, gene_variants
):
    local_blocks = genotypes.shape[1] // BLK
    owned_count = local_blocks // lax.axis_size("samp")
    samp_index = lax.axis_index("samp")
    gene_index = lax.axis_index("gene")
    block_ids = (
        gene_index * local_blocks
        + samp_index * owned_count
        + jnp.arange(owned_count, dtype=jnp.int32)
    )
    variant_blocks = variant_weight.reshape(local_blocks, BLK)
    own_weights = lax.dynamic_slice_in_dim(variant_blocks, samp_index * owned_count, owned_count, 0)
    effective, member = live_weights(block_ids, own_weights, block_gene, gene_variants)
    own_words = lax.all_to_all(genotypes, "samp", split_axis=1, concat_axis=0, tiled=True)
    all_weight, all_residual = (
        lax.all_gather(sample_weight, "samp", axis=1, tiled=True),
        lax.all_gather(residual, "samp", axis=1, tiled=True),
    )
    own_freq = lax.dynamic_slice_in_dim(
        allele_freq, samp_index * owned_count * BLK, owned_count * BLK, 0
    )
    root_all = jnp.sqrt(all_weight)
    weighted_residual = (root_all * all_residual).astype(jnp.bfloat16)
    scaled = unpack(own_words, own_freq, root_all)
    gram_part = block_grams(scaled, owned_count)
    flattened = scaled.reshape(scaled.shape[0] * scaled.shape[1], owned_count * BLK)
    scores = jnp.dot(
        weighted_residual.reshape(1, -1), flattened, preferred_element_type=jnp.float32
    )
    variance = jnp.sum(all_weight * all_residual * all_residual) / (
        all_weight.shape[0] * all_weight.shape[1]
    )
    gene_parts = jnp.dot(
        block_stats(gram_part, scores, effective), member, precision=lax.Precision.HIGHEST
    )
    totals = lax.psum(gene_parts, ("samp", "gene"))
    burden = totals[0] / jnp.sqrt(variance * totals[1])
    skat_score = (totals[2] - variance * totals[3]) / (variance * jnp.sqrt(2.0 * totals[4]))
    return (burden, skat_score)


def solution(mesh):
    placed = (P("samp", "gene"), P("gene"), P(None, "samp"), P(None, "samp"), P("gene"), P(), P())
    return jax.shard_map(local, mesh=mesh, in_specs=placed, out_specs=(P(), P()), check_vma=False)
```

profile of v0, /device:TPU:0, one launch (start us, length us, event | category | flops | bytes accessed | tf_op | source)
XLA Modules:
  0.0 128.4 jit_solution(14625321429608748185)
XLA Ops:
  0.6 0.9 copy-done
  1.5 0.6 copy_bitcast_fusion
  2.2 7.4 %all-to-all-start = ((s32[32,8,128]{2,0,1:T(8,128)}), s32[32,8,128]{2,0,1:T(8,128)S(1)}, u32[]{:S(2)}, u32[]{:S(2)}) async-start(s32[32,8,128]{2,0,1:T(8,128)} %copy_bitcast_fusion), calls=%async_computation | async-start | bytes 262144 | tf_op jit(solution)/shard_map/all_to_all | solution.py:63
  9.7 0.6 fusion.16
  10.3 0.6 fusion.19
  10.9 1.3 fusion.17
  12.2 31.2 %all-gather.1 = f32[8,32,16]{1,2,0:T(8,128)S(1)} all-gather(f32[1,32,16]{1,2,0:T(8,128)S(1)} %bitcast.67), channel_id=1, replica_groups=mesh['samp'=8,'gene'=4] {'samp'}, dimensions={0}, use_global_device_ids=true | all-gather | bytes 18432 | tf_op jit(solution)/shard_map/all_gather | solution.py:66
  43.4 0.1 reshape.172
  43.5 30.5 %all-gather = f32[8,32,16]{1,2,0:T(8,128)S(1)} all-gather(f32[1,32,16]{1,2,0:T(8,128)S(1)} %bitcast.68), channel_id=1, replica_groups=mesh['samp'=8,'gene'=4] {'samp'}, dimensions={0}, use_global_device_ids=true | all-gather | bytes 18432 | tf_op jit(solution)/shard_map/all_gather | solution.py:65
  74.1 0.1 reshape.170
  74.2 0.6 fusion.12
  76.0 0.8 dynamic-slice_multiply_fusion
  76.8 1.3 fusion.18
  78.1 0.1 copy.22
  78.2 0.9 convolution_bitcast_fusion
  79.1 1.2 gather_fusion
  80.4 1.9 %fusion.20 = (f32[]{:T(128)}, f32[1,128]{1,0:T(1,128)S(1)}) fusion(f32[128]{0:T(128)S(1)} %gather_fusion, f32[8,128]{1,0:T(8,128)} %bitcast.70, s32[]{:T(128)S(6)} %select_n.22, s32[]{:T(128)} %fusion.18, s32[]{:T(128)S(6)} %mul.106), kind=kLoop, calls=%fused_computation.37 | loop fusion | flops 767 | bytes 1552 | tf_op jit(solution)/shard_map/reduce_sum | solution.py:29
  82.3 0.8 fusion.11
  83.1 1.2 multiply_reduce_fusion.1
  84.4 0.7 multiply_reduce_fusion
  85.1 3.3 %stack.23 = f32[5,1]{0,1:T(1,128)S(1)} concatenate(f32[1,1]{0,1:T(1,128)} %bitcast.12, f32[1,1]{0,1:T(1,128)} %bitcast.17, f32[1,1]{0,1:T(1,128)} %bitcast.18, f32[1,1]{0,1:T(1,128)} %bitcast.21, f32[1,1]{0,1:T(1,128)} %bitcast.22), dimensions={0} | concatenate | bytes 40 | tf_op jit(solution)/shard_map/stack | solution.py:32
  88.3 0.1 broadcast_multiply_fusion
  88.4 39.5 %psum.7 = f32[5,16]{1,0:T(8,128)S(1)} all-reduce(f32[5,16]{1,0:T(8,128)S(1)} %broadcast_multiply_fusion), channel_id=1, replica_groups=mesh['samp'=8,'gene'=4] {'samp','gene'}, use_global_device_ids=true, to_apply=%region_8.9 | all-reduce | flops 80 | bytes 640 | tf_op jit(solution)/shard_map/psum | solution.py:85
  127.9 0.5 fusion.22
  (14 shorter events, 0.1 us)
Async XLA Ops:
  0.6 0.9 copy-start
  2.2 7.5 %copy-start.3 = (s32[32]{0:T(128)S(1)}, s32[32]{0:T(128)}, u32[]{:S(2)}) copy-start(s32[32]{0:T(128)} %param.12) | copy-start | bytes 388
  2.2 10.0 %copy-start.1 = (f32[16,32]{1,0:T(8,128)S(1)}, f32[16,32]{1,0:T(8,128)}, u32[]{:S(2)}) copy-start(f32[16,32]{1,0:T(8,128)} %param.10) | copy-start | bytes 6148
  2.2 75.9 %all-to-all-start = ((s32[32,8,128]{2,0,1:T(8,128)}), s32[32,8,128]{2,0,1:T(8,128)S(1)}, u32[]{:S(2)}, u32[]{:S(2)}) async-start(s32[32,8,128]{2,0,1:T(8,128)} %copy_bitcast_fusion), calls=%async_computation | async-start | bytes 262144 | tf_op jit(solution)/shard_map/all_to_all | solution.py:63
  12.2 31.3 %copy-start.2 = (f32[16,32]{1,0:T(8,128)S(1)}, f32[16,32]{1,0:T(8,128)}, u32[]{:S(2)}) copy-start(f32[16,32]{1,0:T(8,128)} %param.9) | copy-start | bytes 6148
  74.1 2.7 %copy-start.4 = (s32[16]{0:T(128)S(1)}, s32[16]{0:T(128)}, u32[]{:S(2)}) copy-start(s32[16]{0:T(128)} %param.13) | copy-start | bytes 196
where the time goes:
time: 129 us; the launch traced here: 128 us
  blocking collectives  101 us (78%)
  other arithmetic  8.47 us (7%)
  starting transfers between devices  7.44 us (6%)
  local copies, waits for them, and re-layouts  6.39 us (5%)
  matrix products  2.98 us (2%)
  between operations  1.93 us (1%)
    psum x1, blocking collectives, local(): totals = lax.psum(gene_parts, ('samp', 'gene'))  39.5 us
    all_gather x1, blocking collectives, local(): lax.all_gather(residual, 'samp', axis=1, tiled=True)  31.2 us
    all_gather x1, blocking collectives, local(): lax.all_gather(sample_weight, 'samp', axis=1, tiled=True)  30.5 us
    all_to_all x1, starting transfers between devices, local(): lax.all_to_all(genotypes, 'samp', split_axis=1, concat_axis=0, tiled=True)  7.44 us
    another operation x1, local copies, waits for them, and re-layouts, block_stats(): return jnp.stack([burden_sum, burden_var, skat_sum, trace_one, trace_two])  3.27 us
  transfers between devices with their start and end apart: 1, of which 0 were waited for; matrix products, arithmetic and copies ran while one was open for 4% of the time, Pallas kernels for 0%

commit v1 on v0

--- a/solution.py
+++ b/solution.py
@@ -60,7 +60,12 @@
     variant_blocks = variant_weight.reshape(local_blocks, BLK)
     own_weights = lax.dynamic_slice_in_dim(variant_blocks, samp_index * owned_count, owned_count, 0)
     effective, member = live_weights(block_ids, own_weights, block_gene, gene_variants)
-    own_words = lax.all_to_all(genotypes, "samp", split_axis=1, concat_axis=0, tiled=True)
+    own_words = jnp.concatenate(
+        lax.all_to_all(
+            jnp.stack(jnp.split(genotypes, lax.axis_size("samp"), axis=1)), "samp", 0, 0
+        ),
+        axis=0,
+    )
     all_weight, all_residual = (
         lax.all_gather(sample_weight, "samp", axis=1, tiled=True),
         lax.all_gather(residual, "samp", axis=1, tiled=True),

time: 129 us -> 138 us (1.070)
  local copies, waits for them, and re-layouts: 6.39 us -> 15.4 us
    unnamed x12 -> x17, local copies, waits for them, and re-layouts: 1.08 us -> 9.39 us
where the time goes in v1:
time: 138 us; the launch traced here: 137 us
  blocking collectives  101 us (73%)
  local copies, waits for them, and re-layouts  15.4 us (11%)
  other arithmetic  8.47 us (6%)
  starting transfers between devices  7.44 us (5%)
  matrix products  2.98 us (2%)
  between operations  1.93 us (1%)
    psum x1, blocking collectives, local(): totals = lax.psum(gene_parts, ('samp', 'gene'))  39.5 us
    all_gather x1, blocking collectives, local(): lax.all_gather(residual, 'samp', axis=1, tiled=True)  31.2 us
    all_gather x1, blocking collectives, local(): lax.all_gather(sample_weight, 'samp', axis=1, tiled=True)  30.5 us
    unnamed x17, local copies, waits for them, and re-layouts  9.39 us
    all_to_all x1, starting transfers between devices, local(): lax.all_to_all(jnp.stack(jnp.split(genotypes, lax.axis_size('samp'), axis...  7.44 us
    another operation x1, local copies, waits for them, and re-layouts, block_stats(): return jnp.stack([burden_sum, burden_var, skat_sum, trace_one, trace_two])  3.27 us
  transfers between devices with their start and end apart: 1, of which 0 were waited for; matrix products, arithmetic and copies ran while one was open for 4% of the time, Pallas kernels for 0%

profile of v1, /device:TPU:0, one launch (start us, length us, event | category | flops | bytes accessed | tf_op | source)
XLA Modules:
  0.0 137.4 jit_solution(5467603916590996621)
XLA Ops:
  0.6 1.3 constant_dynamic-update-slice_fusion.7
  1.9 1.3 constant_dynamic-update-slice_fusion.6
  3.3 1.3 constant_dynamic-update-slice_fusion.5
  4.6 1.3 constant_dynamic-update-slice_fusion.4
  5.9 1.3 constant_dynamic-update-slice_fusion.3
  7.2 1.3 constant_dynamic-update-slice_fusion.2
  8.5 1.3 constant_dynamic-update-slice_fusion.1
  9.8 1.3 constant_dynamic-update-slice_fusion
  11.2 7.4 %all-to-all-start = ((s32[8,32,128]{2,1,0:T(8,128)}), s32[8,32,128]{2,1,0:T(8,128)S(1)}, u32[]{:S(2)}, u32[]{:S(2)}) async-start(s32[8,32,128]{2,1,0:T(8,128)} %constant_dynamic-update-slice_fusion), calls=%async_computation | async-start | bytes 262144 | tf_op jit(solution)/shard_map/all_to_all | solution.py:64
  18.6 0.6 fusion.16
  19.3 0.6 fusion.19
  19.9 1.3 fusion.17
  21.2 31.2 %all-gather.1 = f32[8,32,16]{1,2,0:T(8,128)S(1)} all-gather(f32[1,32,16]{1,2,0:T(8,128)S(1)} %bitcast.76), channel_id=1, replica_groups=mesh['samp'=8,'gene'=4] {'samp'}, dimensions={0}, use_global_device_ids=true | all-gather | bytes 18432 | tf_op jit(solution)/shard_map/all_gather | solution.py:71
  52.5 30.5 %all-gather = f32[8,32,16]{1,2,0:T(8,128)S(1)} all-gather(f32[1,32,16]{1,2,0:T(8,128)S(1)} %bitcast.77), channel_id=1, replica_groups=mesh['samp'=8,'gene'=4] {'samp'}, dimensions={0}, use_global_device_ids=true | all-gather | bytes 18432 | tf_op jit(solution)/shard_map/all_gather | solution.py:70
  85.0 0.8 dynamic-slice_multiply_fusion
  85.8 1.3 fusion.18
  87.1 0.9 convolution_bitcast_fusion
  88.1 1.2 gather_fusion
  89.3 1.9 %fusion.20 = (f32[]{:T(128)}, f32[1,128]{1,0:T(1,128)S(1)}) fusion(f32[128]{0:T(128)S(1)} %gather_fusion, f32[8,128]{1,0:T(8,128)} %bitcast.79, s32[]{:T(128)S(6)} %select_n.22, s32[]{:T(128)} %fusion.18, s32[]{:T(128)S(6)} %mul.106), kind=kLoop, calls=%fused_computation.44 | loop fusion | flops 767 | bytes 1552 | tf_op jit(solution)/shard_map/reduce_sum | solution.py:29
  91.3 0.8 fusion.11
  92.1 1.2 multiply_reduce_fusion.1
  93.3 0.7 multiply_reduce_fusion
  94.0 3.3 %stack.59 = f32[5,1]{0,1:T(1,128)S(1)} concatenate(f32[1,1]{0,1:T(1,128)} %bitcast.19, f32[1,1]{0,1:T(1,128)} %bitcast.24, f32[1,1]{0,1:T(1,128)} %bitcast.25, f32[1,1]{0,1:T(1,128)} %bitcast.28, f32[1,1]{0,1:T(1,128)} %bitcast.29), dimensions={0} | concatenate | bytes 40 | tf_op jit(solution)/shard_map/stack | solution.py:32
  97.4 39.5 %psum.7 = f32[5,16]{1,0:T(8,128)S(1)} all-reduce(f32[5,16]{1,0:T(8,128)S(1)} %broadcast_multiply_fusion), channel_id=1, replica_groups=mesh['samp'=8,'gene'=4] {'samp','gene'}, use_global_device_ids=true, to_apply=%region_8.9 | all-reduce | flops 80 | bytes 640 | tf_op jit(solution)/shard_map/psum | solution.py:90
  (19 shorter events, 1.5 us)
Async XLA Ops:
  11.2 7.5 %copy-start.2 = (s32[32]{0:T(128)S(1)}, s32[32]{0:T(128)}, u32[]{:S(2)}) copy-start(s32[32]{0:T(128)} %param.12) | copy-start | bytes 388
  11.2 10.0 %copy-start = (f32[16,32]{1,0:T(8,128)S(1)}, f32[16,32]{1,0:T(8,128)}, u32[]{:S(2)}) copy-start(f32[16,32]{1,0:T(8,128)} %param.10) | copy-start | bytes 6148
  11.2 75.9 %all-to-all-start = ((s32[8,32,128]{2,1,0:T(8,128)}), s32[8,32,128]{2,1,0:T(8,128)S(1)}, u32[]{:S(2)}, u32[]{:S(2)}) async-start(s32[8,32,128]{2,1,0:T(8,128)} %constant_dynamic-update-slice_fusion), calls=%async_computation | async-start | bytes 262144 | tf_op jit(solution)/shard_map/all_to_all | solution.py:64
  21.2 31.3 %copy-start.1 = (f32[16,32]{1,0:T(8,128)S(1)}, f32[16,32]{1,0:T(8,128)}, u32[]{:S(2)}) copy-start(f32[16,32]{1,0:T(8,128)} %param.9) | copy-start | bytes 6148
  83.1 2.7 %copy-start.3 = (s32[16]{0:T(128)S(1)}, s32[16]{0:T(128)}, u32[]{:S(2)}) copy-start(s32[16]{0:T(128)} %param.13) | copy-start | bytes 196
